TPU v7x, 32 devices: a whole 2x2x4 slice. The times are simulated.
32 devices in a mesh: row: 4 (over y, core), col: 8 (over z, x).
Axes of the slice: x: 2, y: 2, z: 4, core: 2. Of those that a mesh axis runs over, the one named last changes fastest.
Arguments:
- nodes: bfloat16 [32768, 512], P(('row', 'col')), may hold values from -8 to 8
- ln1_gain: float32 [512], replicated, may hold values from 0.25 to 1.75
- w_qkv: bfloat16 [512, 1536], replicated, may hold values from -1 to 1
- w_out: bfloat16 [512, 512], replicated, may hold values from -0.25 to 0.25
- ln2_gain: float32 [512], replicated, may hold values from 0.25 to 1.75
- w_up: bfloat16 [512, 2048], replicated, may hold values from -0.25 to 0.25
- w_down: bfloat16 [2048, 512], replicated, may hold values from -0.125 to 0.125
- adjacency: int32 [32768, 128], P(('row', 'col')), may hold values 0 or 1
- remote_ids: int32 [32, 10], replicated, may hold values from 0 to 255, as said below
- remote_live: int32 [32, 10], replicated, may hold values from 0 to 1, as said below
Outputs:
- updated: bfloat16 [32768, 512], P(('row', 'col'))
Inputs may be any that keep to these rules, and one draw needn't show every extreme that they name: `remote_ids`: every entry of device d's list names a block of another device in d's row or d's column of the mesh; the entries of one list are distinct; at most 1 live entries of one list name blocks of one device, and some list has exactly 1 from one device. `remote_live`: some device has all 10 entries live; every device has 8 or more.
All inputs are finite; a program needn't handle non-finite values. No bound on the sum of `adjacency` on one device may be relied on, other than what follows from the above.
Results may differ from a plain program's by a relative error of at most 0.005.
Values may be sent and summed in bfloat16 or wider, within the bound.
A program may use at most 128 MiB of HBM per device.

v0:
```python
import math
import jax
import jax.numpy as jnp
from jax import lax
from jax.sharding import PartitionSpec as P

HEADS = 8
BLK = 128
CAP = 1
EPS = 1e-05
NEG_FILL = -1e30


def normalize(values, gain):
    values = values.astype(jnp.float32)
    row_mean = jnp.mean(values, axis=-1, keepdims=True)
    centered = values - row_mean
    row_var = jnp.mean(centered * centered, axis=-1, keepdims=True)
    return (centered * lax.rsqrt(row_var + EPS) * gain).astype(jnp.bfloat16)


def attend(queries, local_kv, remote_kv, adj_rows, key_alive):
    row_count = queries.shape[0]
    model_width = queries.shape[1]
    head_dim = model_width // HEADS
    block_count = row_count // BLK
    score_scale = 1.0 / math.sqrt(head_dim)
    query_h = queries.reshape(block_count, BLK, HEADS, head_dim)
    local_keys = local_kv[:, :model_width].reshape(block_count, BLK, HEADS, head_dim)
    local_vals = local_kv[:, model_width:].reshape(block_count, BLK, HEADS, head_dim)
    remote_keys = remote_kv[:, :model_width].reshape(-1, HEADS, head_dim)
    remote_vals = remote_kv[:, model_width:].reshape(-1, HEADS, head_dim)
    local_scores = (
        jnp.einsum("bihd,bjhd->bhij", query_h, local_keys, preferred_element_type=jnp.float32)
        * score_scale
    )
    eye_mask = jnp.arange(BLK)[:, None] == jnp.arange(BLK)[None, :]
    allowed = (adj_rows.reshape(block_count, BLK, BLK) > 0) | eye_mask[None]
    local_scores = jnp.where(allowed[:, None], local_scores, NEG_FILL)
    remote_scores = (
        jnp.einsum("bihd,jhd->bhij", query_h, remote_keys, preferred_element_type=jnp.float32)
        * score_scale
    )
    remote_scores = jnp.where(key_alive[None, None, None, :] > 0, remote_scores, NEG_FILL)
    row_max = jnp.maximum(jnp.max(local_scores, axis=-1), jnp.max(remote_scores, axis=-1))
    local_exp = jnp.exp(local_scores - row_max[..., None])
    remote_exp = jnp.exp(remote_scores - row_max[..., None])
    row_total = jnp.sum(local_exp, axis=-1) + jnp.sum(remote_exp, axis=-1)
    local_probs = (local_exp / row_total[..., None]).astype(jnp.bfloat16)
    remote_probs = (remote_exp / row_total[..., None]).astype(jnp.bfloat16)
    summed = jnp.einsum(
        "bhij,bjhd->bihd", local_probs, local_vals, preferred_element_type=jnp.float32
    )
    summed = summed + jnp.einsum(
        "bhij,jhd->bihd", remote_probs, remote_vals, preferred_element_type=jnp.float32
    )
    return summed.reshape(row_count, model_width).astype(jnp.bfloat16)


def choose_blocks(owner_rows, rank_rows, alive_rows, local_rows, self_index):
    cap_iota = jnp.arange(CAP, dtype=jnp.int32)
    matched = (
        alive_rows[:, None, :]
        & (owner_rows[:, None, :] == self_index)
        & (rank_rows[:, None, :] == cap_iota[None, :, None])
    )
    return jnp.sum(matched.astype(jnp.int32) * local_rows[:, None, :], axis=2)


def outgoing(source, chosen_local, peer_count):
    picked = jnp.take(source, chosen_local.reshape(-1), axis=0, mode="clip")
    return picked.reshape(peer_count, CAP, BLK, source.shape[2])


def shards(
    nodes, ln1_gain, w_qkv, w_out, ln2_gain, w_up, w_down, adjacency, remote_ids, remote_live
):
    model_width = nodes.shape[1]
    node_count = nodes.shape[0]
    local_blocks = node_count // BLK
    slot_count = remote_ids.shape[1]
    row_size = lax.axis_size("row")
    col_size = lax.axis_size("col")
    my_row = lax.axis_index("row")
    my_col = lax.axis_index("col")
    self_index = my_row * col_size + my_col
    normed = normalize(nodes, ln1_gain)
    projected = jnp.dot(normed, w_qkv, preferred_element_type=jnp.float32).astype(jnp.bfloat16)
    queries = projected[:, :model_width]
    keyval = projected[:, model_width:]
    owner_dev = remote_ids // local_blocks
    local_slot = remote_ids % local_blocks
    alive_all = remote_live > 0
    same_owner = owner_dev[:, :, None] == owner_dev[:, None, :]
    slot_iota = jnp.arange(slot_count, dtype=jnp.int32)
    earlier = slot_iota[:, None] < slot_iota[None, :]
    slot_rank = jnp.sum(
        (same_owner & earlier[None] & alive_all[:, :, None]).astype(jnp.int32), axis=1
    )
    row_start = my_row * col_size
    col_pick = choose_blocks(
        lax.dynamic_slice_in_dim(owner_dev, row_start, col_size, 0),
        lax.dynamic_slice_in_dim(slot_rank, row_start, col_size, 0),
        lax.dynamic_slice_in_dim(alive_all, row_start, col_size, 0),
        lax.dynamic_slice_in_dim(local_slot, row_start, col_size, 0),
        self_index,
    )

    def column_of(table):
        return lax.dynamic_index_in_dim(
            table.reshape(row_size, col_size, slot_count), my_col, 1, keepdims=False
        )

    row_pick = choose_blocks(
        column_of(owner_dev),
        column_of(slot_rank),
        column_of(alive_all),
        column_of(local_slot),
        self_index,
    )
    source = normed.reshape(local_blocks, BLK, model_width)
    col_recv = lax.all_to_all(
        outgoing(source, col_pick, col_size), "col", split_axis=0, concat_axis=0, tiled=True
    )
    row_recv = lax.all_to_all(
        outgoing(source, row_pick, row_size), "row", split_axis=0, concat_axis=0, tiled=True
    )
    own_owner = lax.dynamic_index_in_dim(owner_dev, self_index, 0, keepdims=False)
    own_rank = jnp.minimum(
        lax.dynamic_index_in_dim(slot_rank, self_index, 0, keepdims=False), CAP - 1
    )
    own_alive = lax.dynamic_index_in_dim(remote_live, self_index, 0, keepdims=False)
    owner_row = own_owner // col_size
    owner_col = own_owner % col_size
    feature_width = col_recv.shape[3]
    from_col = jnp.take(
        col_recv.reshape(col_size * CAP, BLK, feature_width),
        owner_col * CAP + own_rank,
        axis=0,
        mode="clip",
    )
    from_row = jnp.take(
        row_recv.reshape(row_size * CAP, BLK, feature_width),
        owner_row * CAP + own_rank,
        axis=0,
        mode="clip",
    )
    gathered = jnp.where((owner_row == my_row)[:, None, None], from_col, from_row).reshape(
        slot_count * BLK, feature_width
    )
    remote_kv = jnp.dot(
        gathered, w_qkv[:, model_width:], preferred_element_type=jnp.float32
    ).astype(jnp.bfloat16)
    key_alive = jnp.repeat(own_alive, BLK)
    group_rows = 2 * BLK
    group_count = node_count // group_rows

    def one_group(pieces):
        query_part, kv_part, adj_part = pieces
        return attend(query_part, kv_part, remote_kv, adj_part, key_alive)

    mixed = lax.map(
        one_group,
        (
            queries.reshape(group_count, group_rows, model_width),
            keyval.reshape(group_count, group_rows, 2 * model_width),
            adjacency.reshape(group_count, group_rows, BLK),
        ),
    )
    mixed = mixed.reshape(node_count, model_width)
    residual = nodes.astype(jnp.float32) + jnp.dot(mixed, w_out, preferred_element_type=jnp.float32)
    normed_two = normalize(residual, ln2_gain)
    upward = jnp.dot(normed_two, w_up, preferred_element_type=jnp.float32)
    activated = jax.nn.gelu(upward, approximate=True).astype(jnp.bfloat16)
    return (residual + jnp.dot(activated, w_down, preferred_element_type=jnp.float32)).astype(
        jnp.bfloat16
    )


def solution(mesh):
    return jax.shard_map(
        shards,
        mesh=mesh,
        in_specs=(
            P(("row", "col"), None),
            P(),
            P(),
            P(),
            P(),
            P(),
            P(),
            P(("row", "col"), None),
            P(),
            P(),
        ),
        out_specs=P(("row", "col"), None),
        check_vma=False,
    )
```

profile of v0, /device:TPU:0, one launch (start us, length us, event | category | flops | bytes accessed | tf_op | source)
XLA Modules:
  0.0 227.4 jit_solution(1038354618828412443)
XLA Ops:
  9.1 4.3 %all-to-all-start.1 = ((bf16[4,1,128,512]{3,2,1,0:T(8,128)(2,1)}), bf16[4,1,128,512]{3,2,1,0:T(8,128)(2,1)}, u32[]{:S(2)}, u32[]{:S(2)}) async-start(bf16[4,1,128,512]{3,2,1,0:T(8,128)(2,1)} %bitcast.137), calls=%async_computation.1 | async-start | bytes 1048576 | tf_op jit(solution)/shard_map/all_to_all | solution.py:125
  15.1 7.7 %all-to-all-done.1 = bf16[4,1,128,512]{3,2,1,0:T(8,128)(2,1)} async-done(((bf16[4,1,128,512]{3,2,1,0:T(8,128)(2,1)}), bf16[4,1,128,512]{3,2,1,0:T(8,128)(2,1)}, u32[]{:S(2)}, u32[]{:S(2)}) %all-to-all-start.1) | async-done | bytes 524320 | tf_op jit(solution)/shard_map/all_to_all | solution.py:125
  22.9 6.6 %all-to-all-start = ((bf16[8,1,128,512]{3,2,1,0:T(8,128)(2,1)}), bf16[8,1,128,512]{3,2,1,0:T(8,128)(2,1)S(1)}, u32[]{:S(2)}, u32[]{:S(2)}) async-start(bf16[8,1,128,512]{3,2,1,0:T(8,128)(2,1)} %bitcast.135), calls=%async_computation | async-start | bytes 2097152 | tf_op jit(solution)/shard_map/all_to_all | solution.py:122
  29.4 3.6 %convolution_convert_fusion.1 = bf16[1024,1536]{1,0:T(8,128)(2,1)S(1)} fusion(bf16[1024,512]{0,1:T(8,128)(2,1)} %fusion.34, bf16[512,1536]{1,0:T(8,128)(2,1)} %param.14), kind=kOutput, calls=%fused_computation.50 | convolution fusion | flops 1612185600 | bytes 5767168 | tf_op jit(solution)/shard_map/dot_general | solution.py:88
  39.0 16.1 %all-to-all-done = bf16[8,1,128,512]{3,2,1,0:T(8,128)(2,1)S(1)} async-done(((bf16[8,1,128,512]{3,2,1,0:T(8,128)(2,1)}), bf16[8,1,128,512]{3,2,1,0:T(8,128)(2,1)S(1)}, u32[]{:S(2)}, u32[]{:S(2)}) %all-to-all-start) | async-done | bytes 1048608 | tf_op jit(solution)/shard_map/all_to_all | solution.py:122
  59.0 3.0 %convolution_convert_fusion = bf16[1280,1024]{1,0:T(8,128)(2,1)} fusion(bf16[1280,512]{1,0:T(8,128)(2,1)S(1)} %bitcast_select_fusion, bf16[512,1536]{1,0:T(8,128)(2,1)S(1)} %copy-done.11), kind=kOutput, calls=%fused_computation.49 | convolution fusion | flops 1343488000 | bytes 4980736 | tf_op jit(solution)/shard_map/dot_general | solution.py:151
  62.0 4.4 %copy.136 = bf16[1280,1024]{0,1:T(8,128)(2,1)} copy(bf16[1280,1024]{1,0:T(8,128)(2,1)} %convolution_convert_fusion) | data formatting | bytes 5242880
  66.5 147.2 %while.11 = (s32[]{:T(128)}, bf16[4,256,512]{2,1,0:T(8,128)(2,1)}, bf16[4,256,1024]{2,1,0:T(8,128)(2,1)}, s32[4,256,128]{2,1,0:T(8,128)}, bf16[4,256,512]{2,1,0:...) while((s32[]{:T(128)}, bf16[4,256,512]{2,1,0:T(8,128)(2,1)}, ...), condition=%wide.region_10.11_spmd.clone, body=%wide.region_5.10_spmd.clone.sunk | while | flops 772091904 | bytes 101979416 | solution.py:162
  66.5 3.0 %fusion.88 = (bf16[1280,512]{0,1:T(8,128)(2,1)S(1)}, bf16[1280,512]{0,1:T(8,128)(2,1)}) fusion(bf16[1280,1024]{0,1:T(8,128)(2,1)} %get-tuple-element.212), kind=kLoop, calls=%fused_computation.120.clone.1 | loop fusion | bytes 5242880 | tf_op jit(solution)/shard_map/while/body/eval_jaxpr/slice | solution.py:31
  74.7 6.5 %bitcast_reduce_fusion.2 = (f32[2,8,128]{2,0,1:T(2,128)S(1)}, f32[8,2,128,1280]{3,2,1,0:T(8,128)}) fusion(pred[1280]{0:T(1024)(128)(4,1)S(1)} %broadcast_bitcast_fusion.3, bf16[1280,8,64,1]{0,2,3,1:T(8,128)(2,1)S(1)} %bitcast.127, bf16[2,128,8,64]{1,0,3,2:T(2,128)(2,1)} %reshape.378), kind=kOutput, calls=%fused_computation.6.clone.1 | convolution fusion | flops 343406592 | bytes 12068096 | tf_op jit(solution)/shard_map/while/body/eval_jaxpr/bihd,jhd->bhij/dot_general | solution.py:41
  86.8 6.4 %fusion.92 = f32[2,8,128]{2,0,1:T(2,128)S(1)} fusion(f32[8,2,128,1280]{3,2,1,0:T(8,128)} %get-tuple-element.185, f32[2,8,128]{2,0,1:T(2,128)S(1)} %copy.193, pred[1280]{0:T(1024)(128)(4,1)S(1)} %broadcast_bitcast_fusion.3), kind=kLoop, calls=%fused_computation.10.clone.1 | loop fusion | flops 10483712 | bytes 10503424 | tf_op jit(solution)/shard_map/while/body/eval_jaxpr/reduce_sum | solution.py:48
  93.8 4.2 %fusion.93 = f32[2,128,8,64]{1,3,2,0:T(8,128)} fusion(bf16[1280,8,64,1]{0,2,1,3:T(8,128)(2,1)S(1)} %bitcast.129, f32[8,2,128,1280]{3,2,1,0:T(8,128)S(1)} %copy-done.1, f32[2,8,128]{2,0,1:T(2,128)S(1)} %copy.194, f32[2,8,128]{2,0,1:T(2,128)S(1)} %copy.193, pred[1280]{0:T(1024)(128)(4,1)S(1)} %broadcast_bitcast_fusion.3), kind=kOutput, calls=%fused_computation.15.clone.1 | convolution fusion | flops 348651520 | bytes 12338432 | tf_op jit(solution)/shard_map/while/body/eval_jaxpr/bhij,jhd->bihd/dot_general | solution.py:54
  103.3 3.0 %fusion.88 = (bf16[1280,512]{0,1:T(8,128)(2,1)S(1)}, bf16[1280,512]{0,1:T(8,128)(2,1)}) fusion(bf16[1280,1024]{0,1:T(8,128)(2,1)} %get-tuple-element.212), kind=kLoop, calls=%fused_computation.120.clone.1 | loop fusion | bytes 5242880 | tf_op jit(solution)/shard_map/while/body/eval_jaxpr/slice | solution.py:31
  111.5 6.5 %bitcast_reduce_fusion.2 = (f32[2,8,128]{2,0,1:T(2,128)S(1)}, f32[8,2,128,1280]{3,2,1,0:T(8,128)}) fusion(pred[1280]{0:T(1024)(128)(4,1)S(1)} %broadcast_bitcast_fusion.3, bf16[1280,8,64,1]{0,2,3,1:T(8,128)(2,1)S(1)} %bitcast.127, bf16[2,128,8,64]{1,0,3,2:T(2,128)(2,1)} %reshape.378), kind=kOutput, calls=%fused_computation.6.clone.1 | convolution fusion | flops 343406592 | bytes 12068096 | tf_op jit(solution)/shard_map/while/body/eval_jaxpr/bihd,jhd->bhij/dot_general | solution.py:41
  123.6 6.4 %fusion.92 = f32[2,8,128]{2,0,1:T(2,128)S(1)} fusion(f32[8,2,128,1280]{3,2,1,0:T(8,128)} %get-tuple-element.185, f32[2,8,128]{2,0,1:T(2,128)S(1)} %copy.193, pred[1280]{0:T(1024)(128)(4,1)S(1)} %broadcast_bitcast_fusion.3), kind=kLoop, calls=%fused_computation.10.clone.1 | loop fusion | flops 10483712 | bytes 10503424 | tf_op jit(solution)/shard_map/while/body/eval_jaxpr/reduce_sum | solution.py:48
  130.6 4.2 %fusion.93 = f32[2,128,8,64]{1,3,2,0:T(8,128)} fusion(bf16[1280,8,64,1]{0,2,1,3:T(8,128)(2,1)S(1)} %bitcast.129, f32[8,2,128,1280]{3,2,1,0:T(8,128)S(1)} %copy-done.1, f32[2,8,128]{2,0,1:T(2,128)S(1)} %copy.194, f32[2,8,128]{2,0,1:T(2,128)S(1)} %copy.193, pred[1280]{0:T(1024)(128)(4,1)S(1)} %broadcast_bitcast_fusion.3), kind=kOutput, calls=%fused_computation.15.clone.1 | convolution fusion | flops 348651520 | bytes 12338432 | tf_op jit(solution)/shard_map/while/body/eval_jaxpr/bhij,jhd->bihd/dot_general | solution.py:54
  148.3 6.5 %bitcast_reduce_fusion.2 = (f32[2,8,128]{2,0,1:T(2,128)S(1)}, f32[8,2,128,1280]{3,2,1,0:T(8,128)}) fusion(pred[1280]{0:T(1024)(128)(4,1)S(1)} %broadcast_bitcast_fusion.3, bf16[1280,8,64,1]{0,2,3,1:T(8,128)(2,1)S(1)} %bitcast.127, bf16[2,128,8,64]{1,0,3,2:T(2,128)(2,1)} %reshape.378), kind=kOutput, calls=%fused_computation.6.clone.1 | convolution fusion | flops 343406592 | bytes 12068096 | tf_op jit(solution)/shard_map/while/body/eval_jaxpr/bihd,jhd->bhij/dot_general | solution.py:41
  160.4 6.4 %fusion.92 = f32[2,8,128]{2,0,1:T(2,128)S(1)} fusion(f32[8,2,128,1280]{3,2,1,0:T(8,128)} %get-tuple-element.185, f32[2,8,128]{2,0,1:T(2,128)S(1)} %copy.193, pred[1280]{0:T(1024)(128)(4,1)S(1)} %broadcast_bitcast_fusion.3), kind=kLoop, calls=%fused_computation.10.clone.1 | loop fusion | flops 10483712 | bytes 10503424 | tf_op jit(solution)/shard_map/while/body/eval_jaxpr/reduce_sum | solution.py:48
  167.4 4.2 %fusion.93 = f32[2,128,8,64]{1,3,2,0:T(8,128)} fusion(bf16[1280,8,64,1]{0,2,1,3:T(8,128)(2,1)S(1)} %bitcast.129, f32[8,2,128,1280]{3,2,1,0:T(8,128)S(1)} %copy-done.1, f32[2,8,128]{2,0,1:T(2,128)S(1)} %copy.194, f32[2,8,128]{2,0,1:T(2,128)S(1)} %copy.193, pred[1280]{0:T(1024)(128)(4,1)S(1)} %broadcast_bitcast_fusion.3), kind=kOutput, calls=%fused_computation.15.clone.1 | convolution fusion | flops 348651520 | bytes 12338432 | tf_op jit(solution)/shard_map/while/body/eval_jaxpr/bhij,jhd->bihd/dot_general | solution.py:54
  176.8 3.0 %fusion.88 = (bf16[1280,512]{0,1:T(8,128)(2,1)S(1)}, bf16[1280,512]{0,1:T(8,128)(2,1)}) fusion(bf16[1280,1024]{0,1:T(8,128)(2,1)} %get-tuple-element.212), kind=kLoop, calls=%fused_computation.120.clone.1 | loop fusion | bytes 5242880 | tf_op jit(solution)/shard_map/while/body/eval_jaxpr/slice | solution.py:31
  185.1 6.5 %bitcast_reduce_fusion.2 = (f32[2,8,128]{2,0,1:T(2,128)S(1)}, f32[8,2,128,1280]{3,2,1,0:T(8,128)}) fusion(pred[1280]{0:T(1024)(128)(4,1)S(1)} %broadcast_bitcast_fusion.3, bf16[1280,8,64,1]{0,2,3,1:T(8,128)(2,1)S(1)} %bitcast.127, bf16[2,128,8,64]{1,0,3,2:T(2,128)(2,1)} %reshape.378), kind=kOutput, calls=%fused_computation.6.clone.1 | convolution fusion | flops 343406592 | bytes 12068096 | tf_op jit(solution)/shard_map/while/body/eval_jaxpr/bihd,jhd->bhij/dot_general | solution.py:41
  197.2 6.4 %fusion.92 = f32[2,8,128]{2,0,1:T(2,128)S(1)} fusion(f32[8,2,128,1280]{3,2,1,0:T(8,128)} %get-tuple-element.185, f32[2,8,128]{2,0,1:T(2,128)S(1)} %copy.193, pred[1280]{0:T(1024)(128)(4,1)S(1)} %broadcast_bitcast_fusion.3), kind=kLoop, calls=%fused_computation.10.clone.1 | loop fusion | flops 10483712 | bytes 10503424 | tf_op jit(solution)/shard_map/while/body/eval_jaxpr/reduce_sum | solution.py:48
  204.2 4.2 %fusion.93 = f32[2,128,8,64]{1,3,2,0:T(8,128)} fusion(bf16[1280,8,64,1]{0,2,1,3:T(8,128)(2,1)S(1)} %bitcast.129, f32[8,2,128,1280]{3,2,1,0:T(8,128)S(1)} %copy-done.1, f32[2,8,128]{2,0,1:T(2,128)S(1)} %copy.194, f32[2,8,128]{2,0,1:T(2,128)S(1)} %copy.193, pred[1280]{0:T(1024)(128)(4,1)S(1)} %broadcast_bitcast_fusion.3), kind=kOutput, calls=%fused_computation.15.clone.1 | convolution fusion | flops 348651520 | bytes 12338432 | tf_op jit(solution)/shard_map/while/body/eval_jaxpr/bhij,jhd->bihd/dot_general | solution.py:54
  217.8 8.3 %add_convert_fusion = bf16[1024,512]{0,1:T(8,128)(2,1)S(1)} fusion(f32[1024,512]{0,1:T(8,128)} %copy-done.6, bf16[2048,512]{1,0:T(8,128)(2,1)S(1)} %copy-done, bf16[512,2048]{1,0:T(8,128)(2,1)} %param.17, f32[512]{0:T(512)S(1)} %copy-done.12, f32[1024]{0:T(1024)S(1)} %add_rsqrt_fusion, f32[1024]{0:T(1024)S(1)} %broadcast_multiply_fusion), kind=kOutput, calls=%fused_computation.59 | convolution fusion | flops 4316987392 | bytes 7350272 | tf_op jit(solution)/shard_map/dot_general | solution.py:175
  (186 shorter events, 95.3 us)
Async XLA Ops:
  0.0 217.8 %copy-start = (bf16[2048,512]{1,0:T(8,128)(2,1)S(1)}, bf16[2048,512]{1,0:T(8,128)(2,1)}, u32[]{:S(2)}) copy-start(bf16[2048,512]{1,0:T(8,128)(2,1)} %param.18) | copy-start | bytes 6291460
  0.0 2.2 copy-start.10
  2.2 3.6 %copy-start.9 = (s32[32,10]{0,1:T(8,128)S(1)}, s32[32,10]{0,1:T(8,128)}, u32[]{:S(2)}) copy-start(s32[32,10]{0,1:T(8,128)} %param.20) | copy-start | bytes 3844
  2.2 3.8 %copy-start.8 = (s32[32,10]{0,1:T(8,128)S(1)}, s32[32,10]{0,1:T(8,128)}, u32[]{:S(2)}) copy-start(s32[32,10]{0,1:T(8,128)} %param.21) | copy-start | bytes 3844
  5.8 7.7 %copy-start.7 = (bf16[1024,512]{1,0:T(8,128)(2,1)S(1)}, bf16[1024,512]{1,0:T(8,128)(2,1)}, u32[]{:S(2)}) copy-start(bf16[1024,512]{1,0:T(8,128)(2,1)} %copy.143) | copy-start | bytes 3145732
  9.1 13.7 %all-to-all-start.1 = ((bf16[4,1,128,512]{3,2,1,0:T(8,128)(2,1)}), bf16[4,1,128,512]{3,2,1,0:T(8,128)(2,1)}, u32[]{:S(2)}, u32[]{:S(2)}) async-start(bf16[4,1,128,512]{3,2,1,0:T(8,128)(2,1)} %bitcast.137), calls=%async_computation.1 | async-start | bytes 1048576 | tf_op jit(solution)/shard_map/all_to_all | solution.py:125
  22.9 32.2 %all-to-all-start = ((bf16[8,1,128,512]{3,2,1,0:T(8,128)(2,1)}), bf16[8,1,128,512]{3,2,1,0:T(8,128)(2,1)S(1)}, u32[]{:S(2)}, u32[]{:S(2)}) async-start(bf16[8,1,128,512]{3,2,1,0:T(8,128)(2,1)} %bitcast.135), calls=%async_computation | async-start | bytes 2097152 | tf_op jit(solution)/shard_map/all_to_all | solution.py:122
  56.8 2.2 copy-start.11
  81.2 4.0 %copy-start.2 = (bf16[2,128,8,64]{1,0,3,2:T(2,128)(2,1)S(1)}, bf16[2,128,8,64]{1,0,3,2:T(2,128)(2,1)}, u32[]{:S(2)}) copy-start(bf16[2,128,8,64]{1,0,3,2:T(2,128)(2,1)} %reshape.378) | copy-start | bytes 786436 | tf_op jit(solution)/shard_map/while
  85.2 8.0 %copy-start.3 = (bf16[1280,512]{0,1:T(8,128)(2,1)S(1)}, bf16[1280,512]{0,1:T(8,128)(2,1)}, u32[]{:S(2)}) copy-start(bf16[1280,512]{0,1:T(8,128)(2,1)} %get-tuple-element.183) | copy-start | bytes 3932164 | tf_op jit(solution)/shard_map/while
  86.8 7.0 %copy-start.1 = (f32[8,2,128,1280]{3,2,1,0:T(8,128)S(1)}, f32[8,2,128,1280]{3,2,1,0:T(8,128)}, u32[]{:S(2)}) copy-start(f32[8,2,128,1280]{3,2,1,0:T(8,128)} %get-tuple-element.185) | copy-start | bytes 31457284 | tf_op jit(solution)/shard_map/while
  93.8 4.2 %copy-start.5 = (bf16[256,512]{0,1:T(8,128)(2,1)S(1)}, bf16[256,512]{0,1:T(8,128)(2,1)}, u32[]{:S(2)}) copy-start(bf16[256,512]{0,1:T(8,128)(2,1)} %get-tuple-element.190) | copy-start | bytes 786436 | tf_op jit(solution)/shard_map/while
  118.0 4.0 %copy-start.2 = (bf16[2,128,8,64]{1,0,3,2:T(2,128)(2,1)S(1)}, bf16[2,128,8,64]{1,0,3,2:T(2,128)(2,1)}, u32[]{:S(2)}) copy-start(bf16[2,128,8,64]{1,0,3,2:T(2,128)(2,1)} %reshape.378) | copy-start | bytes 786436 | tf_op jit(solution)/shard_map/while
  122.0 8.1 %copy-start.3 = (bf16[1280,512]{0,1:T(8,128)(2,1)S(1)}, bf16[1280,512]{0,1:T(8,128)(2,1)}, u32[]{:S(2)}) copy-start(bf16[1280,512]{0,1:T(8,128)(2,1)} %get-tuple-element.183) | copy-start | bytes 3932164 | tf_op jit(solution)/shard_map/while
  123.6 7.0 %copy-start.1 = (f32[8,2,128,1280]{3,2,1,0:T(8,128)S(1)}, f32[8,2,128,1280]{3,2,1,0:T(8,128)}, u32[]{:S(2)}) copy-start(f32[8,2,128,1280]{3,2,1,0:T(8,128)} %get-tuple-element.185) | copy-start | bytes 31457284 | tf_op jit(solution)/shard_map/while
  130.6 4.2 %copy-start.5 = (bf16[256,512]{0,1:T(8,128)(2,1)S(1)}, bf16[256,512]{0,1:T(8,128)(2,1)}, u32[]{:S(2)}) copy-start(bf16[256,512]{0,1:T(8,128)(2,1)} %get-tuple-element.190) | copy-start | bytes 786436 | tf_op jit(solution)/shard_map/while
  154.8 4.0 %copy-start.2 = (bf16[2,128,8,64]{1,0,3,2:T(2,128)(2,1)S(1)}, bf16[2,128,8,64]{1,0,3,2:T(2,128)(2,1)}, u32[]{:S(2)}) copy-start(bf16[2,128,8,64]{1,0,3,2:T(2,128)(2,1)} %reshape.378) | copy-start | bytes 786436 | tf_op jit(solution)/shard_map/while
  158.8 8.1 %copy-start.3 = (bf16[1280,512]{0,1:T(8,128)(2,1)S(1)}, bf16[1280,512]{0,1:T(8,128)(2,1)}, u32[]{:S(2)}) copy-start(bf16[1280,512]{0,1:T(8,128)(2,1)} %get-tuple-element.183) | copy-start | bytes 3932164 | tf_op jit(solution)/shard_map/while
  160.4 7.0 %copy-start.1 = (f32[8,2,128,1280]{3,2,1,0:T(8,128)S(1)}, f32[8,2,128,1280]{3,2,1,0:T(8,128)}, u32[]{:S(2)}) copy-start(f32[8,2,128,1280]{3,2,1,0:T(8,128)} %get-tuple-element.185) | copy-start | bytes 31457284 | tf_op jit(solution)/shard_map/while
  167.4 4.2 %copy-start.5 = (bf16[256,512]{0,1:T(8,128)(2,1)S(1)}, bf16[256,512]{0,1:T(8,128)(2,1)}, u32[]{:S(2)}) copy-start(bf16[256,512]{0,1:T(8,128)(2,1)} %get-tuple-element.190) | copy-start | bytes 786436 | tf_op jit(solution)/shard_map/while
  191.6 4.0 %copy-start.2 = (bf16[2,128,8,64]{1,0,3,2:T(2,128)(2,1)S(1)}, bf16[2,128,8,64]{1,0,3,2:T(2,128)(2,1)}, u32[]{:S(2)}) copy-start(bf16[2,128,8,64]{1,0,3,2:T(2,128)(2,1)} %reshape.378) | copy-start | bytes 786436 | tf_op jit(solution)/shard_map/while
  195.6 8.1 %copy-start.3 = (bf16[1280,512]{0,1:T(8,128)(2,1)S(1)}, bf16[1280,512]{0,1:T(8,128)(2,1)}, u32[]{:S(2)}) copy-start(bf16[1280,512]{0,1:T(8,128)(2,1)} %get-tuple-element.183) | copy-start | bytes 3932164 | tf_op jit(solution)/shard_map/while
  197.2 7.0 %copy-start.1 = (f32[8,2,128,1280]{3,2,1,0:T(8,128)S(1)}, f32[8,2,128,1280]{3,2,1,0:T(8,128)}, u32[]{:S(2)}) copy-start(f32[8,2,128,1280]{3,2,1,0:T(8,128)} %get-tuple-element.185) | copy-start | bytes 31457284 | tf_op jit(solution)/shard_map/while
  204.2 4.2 %copy-start.5 = (bf16[256,512]{0,1:T(8,128)(2,1)S(1)}, bf16[256,512]{0,1:T(8,128)(2,1)}, u32[]{:S(2)}) copy-start(bf16[256,512]{0,1:T(8,128)(2,1)} %get-tuple-element.190) | copy-start | bytes 786436 | tf_op jit(solution)/shard_map/while
  (3 other events, 4.9 us)
where the time goes:
time: 229 us; the launch traced here: 227 us
  local copies, waits for them, and re-layouts  82.4 us (36%)
  matrix products  74.7 us (33%)
  other arithmetic  35 us (15%)
  waiting for transfers between devices  23.8 us (10%)
  starting transfers between devices  10.8 us (5%)
    dot_general x4, matrix products, attend(): jnp.einsum('bihd,jhd->bhij', query_h, remote_keys, preferred_element_type...  26.2 us
    reduce_sum x8, other arithmetic, attend(): row_total = jnp.sum(local_exp, axis=-1) + jnp.sum(remote_exp, axis=-1)  26.2 us
    dynamic_slice x16, local copies, waits for them, and re-layouts, shards(): lax.map(one_group, (queries.reshape(group_count, group_rows, model_width)...  19.1 us
    dot_general x4, matrix products, attend(): jnp.einsum('bhij,jhd->bihd', remote_probs, remote_vals, preferred_element...  16.9 us
    all_to_all x1, waiting for transfers between devices, shards(): lax.all_to_all(outgoing(source, col_pick, col_size), 'col', split_axis=0,...  16.1 us
    slice x4, local copies, waits for them, and re-layouts, attend(): remote_keys = remote_kv[:, :model_width].reshape(-1, HEADS, head_dim)  11.9 us
    dynamic_update_slice x12, local copies, waits for them, and re-layouts, shards(): lax.map(one_group, (queries.reshape(group_count, group_rows, model_width)...  9.18 us
    dot_general x4, matrix products, attend(): jnp.einsum('bhij,bjhd->bihd', local_probs, local_vals, preferred_element_...  8.63 us
  transfers between devices with their start and end apart: 2, of which 2 were waited for; matrix products, arithmetic and copies ran while one was open for 5% of the time, Pallas kernels for 0%

commit v1 on v0

--- a/solution.py
+++ b/solution.py
@@ -9,6 +9,28 @@
 CAP = 1
 EPS = 1e-05
 NEG_FILL = -1e30
+
+
+def in_blocks(array, dim, count):
+    before, after = (array.shape[:dim], array.shape[dim + 1 :])
+    return jnp.moveaxis(array.reshape(*before, count, -1, *after), dim, 0)
+
+
+def laid_out(pieces, dim):
+    pieces = jnp.moveaxis(pieces, 0, dim)
+    shape = pieces.shape
+    return pieces.reshape(*shape[:dim], shape[dim] * shape[dim + 1], *shape[dim + 2 :])
+
+
+def exchange_directly(x, axis, split_dim, concat_dim):
+    size, index = (lax.axis_size(axis), lax.axis_index(axis))
+    blocks = in_blocks(x, split_dim, size)
+    gathered = [blocks[index]]
+    for turn in range(1, size):
+        sent = blocks[(index + turn) % size]
+        gathered.append(lax.ppermute(sent, axis, [(i, (i + turn) % size) for i in range(size)]))
+    blocks = jnp.stack(gathered)[(index - jnp.arange(size)) % size]
+    return laid_out(blocks, concat_dim)
 
 
 def normalize(values, gain):
@@ -122,9 +144,7 @@
     col_recv = lax.all_to_all(
         outgoing(source, col_pick, col_size), "col", split_axis=0, concat_axis=0, tiled=True
     )
-    row_recv = lax.all_to_all(
-        outgoing(source, row_pick, row_size), "row", split_axis=0, concat_axis=0, tiled=True
-    )
+    row_recv = exchange_directly(outgoing(source, row_pick, row_size), "row", 0, 0)
     own_owner = lax.dynamic_index_in_dim(owner_dev, self_index, 0, keepdims=False)
     own_rank = jnp.minimum(
         lax.dynamic_index_in_dim(slot_rank, self_index, 0, keepdims=False), CAP - 1

time: 229 us -> 217 us (0.948)
  waiting for transfers between devices: 23.8 us -> 7.41 us
  local copies, waits for them, and re-layouts: 82.4 us -> 87 us
    all_to_all x1, waiting for transfers between devices: 16.1 us -> 7.4 us  [shards(): lax.all_to_all(outgoing(source, col_pick, col_size), 'col', split_axis=0,...]
    all_to_all x1 -> x0, waiting for transfers between devices: 7.71 us -> none  [shards(): lax.all_to_all(outgoing(source, row_pick, row_size), 'row', split_axis=0,...]
    all_to_all x1 -> x0, starting transfers between devices: 4.27 us -> none  [shards(): lax.all_to_all(outgoing(source, row_pick, row_size), 'row', split_axis=0,...]
    unnamed x20 -> x22, local copies, waits for them, and re-layouts: 7.54 us -> 7.48 us
  transfers between devices with their start and end apart: 2 -> 4, of which waited for: 2 -> 1; matrix products, arithmetic and copies ran while one was open for 5% -> 8% of each run, Pallas kernels for 0% -> 0%
where the time goes in v1:
time: 217 us; the launch traced here: 215 us
  local copies, waits for them, and re-layouts  87 us (40%)
  matrix products  76.3 us (35%)
  other arithmetic  34.7 us (16%)
  starting transfers between devices  9.09 us (4%)
  waiting for transfers between devices  7.41 us (3%)
    dot_general x4, matrix products, attend(): jnp.einsum('bihd,jhd->bhij', query_h, remote_keys, preferred_element_type...  26.2 us
    reduce_sum x8, other arithmetic, attend(): row_total = jnp.sum(local_exp, axis=-1) + jnp.sum(remote_exp, axis=-1)  26.2 us
    dynamic_slice x16, local copies, waits for them, and re-layouts, shards(): lax.map(one_group, (queries.reshape(group_count, group_rows, model_width)...  19.1 us
    dot_general x4, matrix products, attend(): jnp.einsum('bhij,jhd->bihd', remote_probs, remote_vals, preferred_element...  16.9 us
    slice x4, local copies, waits for them, and re-layouts, attend(): remote_keys = remote_kv[:, :model_width].reshape(-1, HEADS, head_dim)  11.9 us
    dynamic_update_slice x12, local copies, waits for them, and re-layouts, shards(): lax.map(one_group, (queries.reshape(group_count, group_rows, model_width)...  9.18 us
    dot_general x4, matrix products, attend(): jnp.einsum('bhij,bjhd->bihd', local_probs, local_vals, preferred_element_...  8.63 us
    dot_general x1, matrix products, shards(): jnp.dot(activated, w_down, preferred_element_type=jnp.float32)  8.26 us
  transfers between devices with their start and end apart: 4, of which 1 were waited for; matrix products, arithmetic and copies ran while one was open for 8% of the time, Pallas kernels for 0%

profile of v1, /device:TPU:0, one launch (start us, length us, event | category | flops | bytes accessed | tf_op | source)
XLA Modules:
  0.0 215.3 jit_solution(1862576431300966368)
XLA Ops:
  9.0 7.3 %all-to-all-start = ((bf16[8,1,128,512]{3,2,1,0:T(8,128)(2,1)}), bf16[8,1,128,512]{3,2,1,0:T(8,128)(2,1)}, u32[]{:S(2)}, u32[]{:S(2)}) async-start(bf16[8,1,128,512]{3,2,1,0:T(8,128)(2,1)} %bitcast.145), calls=%async_computation | async-start | bytes 2097152 | tf_op jit(solution)/shard_map/all_to_all | solution.py:144
  21.5 5.2 %convolution_convert_fusion.1 = bf16[1024,1536]{1,0:T(8,128)(2,1)} fusion(bf16[1024,512]{0,1:T(8,128)(2,1)} %fusion.34, bf16[512,1536]{1,0:T(8,128)(2,1)} %param.14), kind=kOutput, calls=%fused_computation.51 | convolution fusion | flops 1612185600 | bytes 5767168 | tf_op jit(solution)/shard_map/dot_general | solution.py:110
  26.7 3.1 %slice.40 = bf16[1024,1024]{1,0:T(8,128)(2,1)} slice(bf16[1024,1536]{1,0:T(8,128)(2,1)} %convolution_convert_fusion.1), slice={[0:1024], [512:1536]} | slice | bytes 4194304 | tf_op jit(solution)/shard_map/slice | solution.py:112
  34.7 7.4 %all-to-all-done = bf16[8,1,128,512]{3,2,1,0:T(8,128)(2,1)} async-done(((bf16[8,1,128,512]{3,2,1,0:T(8,128)(2,1)}), bf16[8,1,128,512]{3,2,1,0:T(8,128)(2,1)}, u32[]{:S(2)}, u32[]{:S(2)}) %all-to-all-start) | async-done | bytes 1048608 | tf_op jit(solution)/shard_map/all_to_all | solution.py:144
  42.1 3.0 %gather_fusion.1 = bf16[10,128,512]{2,1,0:T(8,128)(2,1)} fusion(bf16[8,128,512]{2,1,0:T(8,128)(2,1)} %bitcast.6, s32[1024]{0:T(1024)S(1)} %pad_clamp_fusion.3), kind=kCustom, calls=%fused_computation.1 | custom fusion | bytes 2621480 | tf_op jit(solution)/shard_map/jit(_take)/gather | solution.py:156
  47.0 3.0 %convolution_convert_fusion = bf16[1280,1024]{1,0:T(8,128)(2,1)} fusion(bf16[1280,512]{1,0:T(8,128)(2,1)S(1)} %bitcast_select_fusion, bf16[512,1536]{1,0:T(8,128)(2,1)S(1)} %copy-done.12), kind=kOutput, calls=%fused_computation.50 | convolution fusion | flops 1343488000 | bytes 4980736 | tf_op jit(solution)/shard_map/dot_general | solution.py:171
  50.0 4.4 %copy.133 = bf16[1280,1024]{0,1:T(8,128)(2,1)} copy(bf16[1280,1024]{1,0:T(8,128)(2,1)} %convolution_convert_fusion) | data formatting | bytes 5242880
  54.4 147.2 %while.11 = (s32[]{:T(128)}, bf16[4,256,512]{2,1,0:T(8,128)(2,1)}, bf16[4,256,1024]{2,1,0:T(8,128)(2,1)}, s32[4,256,128]{2,1,0:T(8,128)}, bf16[4,256,512]{2,1,0:...) while((s32[]{:T(128)}, bf16[4,256,512]{2,1,0:T(8,128)(2,1)}, ...), condition=%wide.region_10.11_spmd.clone, body=%wide.region_5.10_spmd.clone.sunk | while | flops 772091904 | bytes 101979416 | solution.py:182
  54.4 3.0 %fusion.90 = (bf16[1280,512]{0,1:T(8,128)(2,1)S(1)}, bf16[1280,512]{0,1:T(8,128)(2,1)}) fusion(bf16[1280,1024]{0,1:T(8,128)(2,1)} %get-tuple-element.216), kind=kLoop, calls=%fused_computation.133.clone.1 | loop fusion | bytes 5242880 | tf_op jit(solution)/shard_map/while/body/eval_jaxpr/slice | solution.py:53
  62.6 6.5 %bitcast_reduce_fusion.2 = (f32[2,8,128]{2,0,1:T(2,128)S(1)}, f32[8,2,128,1280]{3,2,1,0:T(8,128)}) fusion(pred[1280]{0:T(1024)(128)(4,1)S(1)} %broadcast_bitcast_fusion.3, bf16[1280,8,64,1]{0,2,3,1:T(8,128)(2,1)S(1)} %bitcast.138, bf16[2,128,8,64]{1,0,3,2:T(2,128)(2,1)} %reshape.441), kind=kOutput, calls=%fused_computation.7.clone.1 | convolution fusion | flops 343406592 | bytes 12068096 | tf_op jit(solution)/shard_map/while/body/eval_jaxpr/bihd,jhd->bhij/dot_general | solution.py:63
  74.8 6.4 %fusion.94 = f32[2,8,128]{2,0,1:T(2,128)S(1)} fusion(f32[8,2,128,1280]{3,2,1,0:T(8,128)} %get-tuple-element.189, f32[2,8,128]{2,0,1:T(2,128)S(1)} %copy.190, pred[1280]{0:T(1024)(128)(4,1)S(1)} %broadcast_bitcast_fusion.3), kind=kLoop, calls=%fused_computation.11.clone.1 | loop fusion | flops 10483712 | bytes 10503424 | tf_op jit(solution)/shard_map/while/body/eval_jaxpr/reduce_sum | solution.py:70
  81.7 4.2 %fusion.95 = f32[2,128,8,64]{1,3,2,0:T(8,128)} fusion(bf16[1280,8,64,1]{0,2,1,3:T(8,128)(2,1)S(1)} %bitcast.140, f32[8,2,128,1280]{3,2,1,0:T(8,128)S(1)} %copy-done.1, f32[2,8,128]{2,0,1:T(2,128)S(1)} %copy.191, f32[2,8,128]{2,0,1:T(2,128)S(1)} %copy.190, pred[1280]{0:T(1024)(128)(4,1)S(1)} %broadcast_bitcast_fusion.3), kind=kOutput, calls=%fused_computation.16.clone.1 | convolution fusion | flops 348651520 | bytes 12338432 | tf_op jit(solution)/shard_map/while/body/eval_jaxpr/bhij,jhd->bihd/dot_general | solution.py:76
  91.2 3.0 %fusion.90 = (bf16[1280,512]{0,1:T(8,128)(2,1)S(1)}, bf16[1280,512]{0,1:T(8,128)(2,1)}) fusion(bf16[1280,1024]{0,1:T(8,128)(2,1)} %get-tuple-element.216), kind=kLoop, calls=%fused_computation.133.clone.1 | loop fusion | bytes 5242880 | tf_op jit(solution)/shard_map/while/body/eval_jaxpr/slice | solution.py:53
  99.4 6.5 %bitcast_reduce_fusion.2 = (f32[2,8,128]{2,0,1:T(2,128)S(1)}, f32[8,2,128,1280]{3,2,1,0:T(8,128)}) fusion(pred[1280]{0:T(1024)(128)(4,1)S(1)} %broadcast_bitcast_fusion.3, bf16[1280,8,64,1]{0,2,3,1:T(8,128)(2,1)S(1)} %bitcast.138, bf16[2,128,8,64]{1,0,3,2:T(2,128)(2,1)} %reshape.441), kind=kOutput, calls=%fused_computation.7.clone.1 | convolution fusion | flops 343406592 | bytes 12068096 | tf_op jit(solution)/shard_map/while/body/eval_jaxpr/bihd,jhd->bhij/dot_general | solution.py:63
  111.6 6.4 %fusion.94 = f32[2,8,128]{2,0,1:T(2,128)S(1)} fusion(f32[8,2,128,1280]{3,2,1,0:T(8,128)} %get-tuple-element.189, f32[2,8,128]{2,0,1:T(2,128)S(1)} %copy.190, pred[1280]{0:T(1024)(128)(4,1)S(1)} %broadcast_bitcast_fusion.3), kind=kLoop, calls=%fused_computation.11.clone.1 | loop fusion | flops 10483712 | bytes 10503424 | tf_op jit(solution)/shard_map/while/body/eval_jaxpr/reduce_sum | solution.py:70
  118.5 4.2 %fusion.95 = f32[2,128,8,64]{1,3,2,0:T(8,128)} fusion(bf16[1280,8,64,1]{0,2,1,3:T(8,128)(2,1)S(1)} %bitcast.140, f32[8,2,128,1280]{3,2,1,0:T(8,128)S(1)} %copy-done.1, f32[2,8,128]{2,0,1:T(2,128)S(1)} %copy.191, f32[2,8,128]{2,0,1:T(2,128)S(1)} %copy.190, pred[1280]{0:T(1024)(128)(4,1)S(1)} %broadcast_bitcast_fusion.3), kind=kOutput, calls=%fused_computation.16.clone.1 | convolution fusion | flops 348651520 | bytes 12338432 | tf_op jit(solution)/shard_map/while/body/eval_jaxpr/bhij,jhd->bihd/dot_general | solution.py:76
  128.0 3.0 %fusion.90 = (bf16[1280,512]{0,1:T(8,128)(2,1)S(1)}, bf16[1280,512]{0,1:T(8,128)(2,1)}) fusion(bf16[1280,1024]{0,1:T(8,128)(2,1)} %get-tuple-element.216), kind=kLoop, calls=%fused_computation.133.clone.1 | loop fusion | bytes 5242880 | tf_op jit(solution)/shard_map/while/body/eval_jaxpr/slice | solution.py:53
  136.2 6.5 %bitcast_reduce_fusion.2 = (f32[2,8,128]{2,0,1:T(2,128)S(1)}, f32[8,2,128,1280]{3,2,1,0:T(8,128)}) fusion(pred[1280]{0:T(1024)(128)(4,1)S(1)} %broadcast_bitcast_fusion.3, bf16[1280,8,64,1]{0,2,3,1:T(8,128)(2,1)S(1)} %bitcast.138, bf16[2,128,8,64]{1,0,3,2:T(2,128)(2,1)} %reshape.441), kind=kOutput, calls=%fused_computation.7.clone.1 | convolution fusion | flops 343406592 | bytes 12068096 | tf_op jit(solution)/shard_map/while/body/eval_jaxpr/bihd,jhd->bhij/dot_general | solution.py:63
  148.4 6.4 %fusion.94 = f32[2,8,128]{2,0,1:T(2,128)S(1)} fusion(f32[8,2,128,1280]{3,2,1,0:T(8,128)} %get-tuple-element.189, f32[2,8,128]{2,0,1:T(2,128)S(1)} %copy.190, pred[1280]{0:T(1024)(128)(4,1)S(1)} %broadcast_bitcast_fusion.3), kind=kLoop, calls=%fused_computation.11.clone.1 | loop fusion | flops 10483712 | bytes 10503424 | tf_op jit(solution)/shard_map/while/body/eval_jaxpr/reduce_sum | solution.py:70
  155.3 4.2 %fusion.95 = f32[2,128,8,64]{1,3,2,0:T(8,128)} fusion(bf16[1280,8,64,1]{0,2,1,3:T(8,128)(2,1)S(1)} %bitcast.140, f32[8,2,128,1280]{3,2,1,0:T(8,128)S(1)} %copy-done.1, f32[2,8,128]{2,0,1:T(2,128)S(1)} %copy.191, f32[2,8,128]{2,0,1:T(2,128)S(1)} %copy.190, pred[1280]{0:T(1024)(128)(4,1)S(1)} %broadcast_bitcast_fusion.3), kind=kOutput, calls=%fused_computation.16.clone.1 | convolution fusion | flops 348651520 | bytes 12338432 | tf_op jit(solution)/shard_map/while/body/eval_jaxpr/bhij,jhd->bihd/dot_general | solution.py:76
  173.0 6.5 %bitcast_reduce_fusion.2 = (f32[2,8,128]{2,0,1:T(2,128)S(1)}, f32[8,2,128,1280]{3,2,1,0:T(8,128)}) fusion(pred[1280]{0:T(1024)(128)(4,1)S(1)} %broadcast_bitcast_fusion.3, bf16[1280,8,64,1]{0,2,3,1:T(8,128)(2,1)S(1)} %bitcast.138, bf16[2,128,8,64]{1,0,3,2:T(2,128)(2,1)} %reshape.441), kind=kOutput, calls=%fused_computation.7.clone.1 | convolution fusion | flops 343406592 | bytes 12068096 | tf_op jit(solution)/shard_map/while/body/eval_jaxpr/bihd,jhd->bhij/dot_general | solution.py:63
  185.2 6.4 %fusion.94 = f32[2,8,128]{2,0,1:T(2,128)S(1)} fusion(f32[8,2,128,1280]{3,2,1,0:T(8,128)} %get-tuple-element.189, f32[2,8,128]{2,0,1:T(2,128)S(1)} %copy.190, pred[1280]{0:T(1024)(128)(4,1)S(1)} %broadcast_bitcast_fusion.3), kind=kLoop, calls=%fused_computation.11.clone.1 | loop fusion | flops 10483712 | bytes 10503424 | tf_op jit(solution)/shard_map/while/body/eval_jaxpr/reduce_sum | solution.py:70
  192.1 4.2 %fusion.95 = f32[2,128,8,64]{1,3,2,0:T(8,128)} fusion(bf16[1280,8,64,1]{0,2,1,3:T(8,128)(2,1)S(1)} %bitcast.140, f32[8,2,128,1280]{3,2,1,0:T(8,128)S(1)} %copy-done.1, f32[2,8,128]{2,0,1:T(2,128)S(1)} %copy.191, f32[2,8,128]{2,0,1:T(2,128)S(1)} %copy.190, pred[1280]{0:T(1024)(128)(4,1)S(1)} %broadcast_bitcast_fusion.3), kind=kOutput, calls=%fused_computation.16.clone.1 | convolution fusion | flops 348651520 | bytes 12338432 | tf_op jit(solution)/shard_map/while/body/eval_jaxpr/bhij,jhd->bihd/dot_general | solution.py:76
  205.7 8.3 %add_convert_fusion = bf16[1024,512]{0,1:T(8,128)(2,1)S(1)} fusion(f32[1024,512]{0,1:T(8,128)} %copy-done.6, bf16[2048,512]{1,0:T(8,128)(2,1)S(1)} %copy-done, bf16[512,2048]{1,0:T(8,128)(2,1)} %param.17, f32[512]{0:T(512)S(1)} %copy-done.13, f32[1024]{0:T(1024)S(1)} %add_rsqrt_fusion, f32[1024]{0:T(1024)S(1)} %broadcast_multiply_fusion), kind=kOutput, calls=%fused_computation.60 | convolution fusion | flops 4316987392 | bytes 7350272 | tf_op jit(solution)/shard_map/dot_general | solution.py:195
  (197 shorter events, 95.4 us)
Async XLA Ops:
  0.0 205.7 %copy-start = (bf16[2048,512]{1,0:T(8,128)(2,1)S(1)}, bf16[2048,512]{1,0:T(8,128)(2,1)}, u32[]{:S(2)}) copy-start(bf16[2048,512]{1,0:T(8,128)(2,1)} %param.18) | copy-start | bytes 6291460
  2.2 3.6 %copy-start.9 = (s32[32,10]{0,1:T(8,128)S(1)}, s32[32,10]{0,1:T(8,128)}, u32[]{:S(2)}) copy-start(s32[32,10]{0,1:T(8,128)} %param.21) | copy-start | bytes 3844
  6.1 10.8 %copy-start.7 = (bf16[1024,512]{1,0:T(8,128)(2,1)S(1)}, bf16[1024,512]{1,0:T(8,128)(2,1)}, u32[]{:S(2)}) copy-start(bf16[1024,512]{1,0:T(8,128)(2,1)} %copy.140) | copy-start | bytes 3145732
  9.0 33.2 %all-to-all-start = ((bf16[8,1,128,512]{3,2,1,0:T(8,128)(2,1)}), bf16[8,1,128,512]{3,2,1,0:T(8,128)(2,1)}, u32[]{:S(2)}, u32[]{:S(2)}) async-start(bf16[8,1,128,512]{3,2,1,0:T(8,128)(2,1)} %bitcast.145), calls=%async_computation | async-start | bytes 2097152 | tf_op jit(solution)/shard_map/all_to_all | solution.py:144
  19.4 12.9 %collective-permute-start.2 = (bf16[1,1,128,512]{3,2,1,0:T(8,128)(2,1)S(1)}, bf16[1,1,128,512]{3,2,1,0:T(8,128)(2,1)S(1)}, u32[]{:S(2)}, u32[]{:S(2)}) collective-permute-start(bf16[1,1,128,512]{3,2,1,0:T(8,128)(2,1)S(1)} %get-tuple-element.127), channel_id=1, source_target_pairs={{0,24},{8,0},{16,8},{24,16},{1,25},{9,1},{17,9},{25,17},{2,26},{10... | collective-permute-start | bytes 393224 | tf_op jit(solution)/shard_map/ppermute | solution.py:31
  20.1 12.2 %collective-permute-start.1 = (bf16[1,1,128,512]{3,2,1,0:T(8,128)(2,1)S(1)}, bf16[1,1,128,512]{3,2,1,0:T(8,128)(2,1)S(1)}, u32[]{:S(2)}, u32[]{:S(2)}) collective-permute-start(bf16[1,1,128,512]{3,2,1,0:T(8,128)(2,1)S(1)} %get-tuple-element.125), channel_id=1, source_target_pairs={{0,16},{8,24},{16,0},{24,8},{1,17},{9,25},{17,1},{25,9},{2,18},{10... | collective-permute-start | bytes 393224 | tf_op jit(solution)/shard_map/ppermute | solution.py:31
  21.0 11.3 %collective-permute-start = (bf16[1,1,128,512]{3,2,1,0:T(8,128)(2,1)S(1)}, bf16[1,1,128,512]{3,2,1,0:T(8,128)(2,1)S(1)}, u32[]{:S(2)}, u32[]{:S(2)}) collective-permute-start(bf16[1,1,128,512]{3,2,1,0:T(8,128)(2,1)S(1)} %get-tuple-element.126), channel_id=1, source_target_pairs={{0,8},{8,16},{16,24},{24,0},{1,9},{9,17},{17,25},{25,1},{2,10},{10... | collective-permute-start | bytes 393224 | tf_op jit(solution)/shard_map/ppermute | solution.py:31
  34.7 10.4 %copy-start.8 = (bf16[10,128,512]{2,1,0:T(8,128)(2,1)S(1)}, bf16[10,128,512]{2,1,0:T(8,128)(2,1)}, u32[]{:S(2)}) copy-start(bf16[10,128,512]{2,1,0:T(8,128)(2,1)} %gather_fusion.4) | copy-start | bytes 3932164
  69.2 4.0 %copy-start.2 = (bf16[2,128,8,64]{1,0,3,2:T(2,128)(2,1)S(1)}, bf16[2,128,8,64]{1,0,3,2:T(2,128)(2,1)}, u32[]{:S(2)}) copy-start(bf16[2,128,8,64]{1,0,3,2:T(2,128)(2,1)} %reshape.441) | copy-start | bytes 786436 | tf_op jit(solution)/shard_map/while
  73.2 8.0 %copy-start.3 = (bf16[1280,512]{0,1:T(8,128)(2,1)S(1)}, bf16[1280,512]{0,1:T(8,128)(2,1)}, u32[]{:S(2)}) copy-start(bf16[1280,512]{0,1:T(8,128)(2,1)} %get-tuple-element.187) | copy-start | bytes 3932164 | tf_op jit(solution)/shard_map/while
  74.8 7.0 %copy-start.1 = (f32[8,2,128,1280]{3,2,1,0:T(8,128)S(1)}, f32[8,2,128,1280]{3,2,1,0:T(8,128)}, u32[]{:S(2)}) copy-start(f32[8,2,128,1280]{3,2,1,0:T(8,128)} %get-tuple-element.189) | copy-start | bytes 31457284 | tf_op jit(solution)/shard_map/while
  81.7 4.2 %copy-start.5 = (bf16[256,512]{0,1:T(8,128)(2,1)S(1)}, bf16[256,512]{0,1:T(8,128)(2,1)}, u32[]{:S(2)}) copy-start(bf16[256,512]{0,1:T(8,128)(2,1)} %get-tuple-element.194) | copy-start | bytes 786436 | tf_op jit(solution)/shard_map/while
  106.0 4.0 %copy-start.2 = (bf16[2,128,8,64]{1,0,3,2:T(2,128)(2,1)S(1)}, bf16[2,128,8,64]{1,0,3,2:T(2,128)(2,1)}, u32[]{:S(2)}) copy-start(bf16[2,128,8,64]{1,0,3,2:T(2,128)(2,1)} %reshape.441) | copy-start | bytes 786436 | tf_op jit(solution)/shard_map/while
  110.0 8.1 %copy-start.3 = (bf16[1280,512]{0,1:T(8,128)(2,1)S(1)}, bf16[1280,512]{0,1:T(8,128)(2,1)}, u32[]{:S(2)}) copy-start(bf16[1280,512]{0,1:T(8,128)(2,1)} %get-tuple-element.187) | copy-start | bytes 3932164 | tf_op jit(solution)/shard_map/while
  111.6 7.0 %copy-start.1 = (f32[8,2,128,1280]{3,2,1,0:T(8,128)S(1)}, f32[8,2,128,1280]{3,2,1,0:T(8,128)}, u32[]{:S(2)}) copy-start(f32[8,2,128,1280]{3,2,1,0:T(8,128)} %get-tuple-element.189) | copy-start | bytes 31457284 | tf_op jit(solution)/shard_map/while
  118.5 4.2 %copy-start.5 = (bf16[256,512]{0,1:T(8,128)(2,1)S(1)}, bf16[256,512]{0,1:T(8,128)(2,1)}, u32[]{:S(2)}) copy-start(bf16[256,512]{0,1:T(8,128)(2,1)} %get-tuple-element.194) | copy-start | bytes 786436 | tf_op jit(solution)/shard_map/while
  142.8 4.0 %copy-start.2 = (bf16[2,128,8,64]{1,0,3,2:T(2,128)(2,1)S(1)}, bf16[2,128,8,64]{1,0,3,2:T(2,128)(2,1)}, u32[]{:S(2)}) copy-start(bf16[2,128,8,64]{1,0,3,2:T(2,128)(2,1)} %reshape.441) | copy-start | bytes 786436 | tf_op jit(solution)/shard_map/while
  146.7 8.1 %copy-start.3 = (bf16[1280,512]{0,1:T(8,128)(2,1)S(1)}, bf16[1280,512]{0,1:T(8,128)(2,1)}, u32[]{:S(2)}) copy-start(bf16[1280,512]{0,1:T(8,128)(2,1)} %get-tuple-element.187) | copy-start | bytes 3932164 | tf_op jit(solution)/shard_map/while
  148.4 7.0 %copy-start.1 = (f32[8,2,128,1280]{3,2,1,0:T(8,128)S(1)}, f32[8,2,128,1280]{3,2,1,0:T(8,128)}, u32[]{:S(2)}) copy-start(f32[8,2,128,1280]{3,2,1,0:T(8,128)} %get-tuple-element.189) | copy-start | bytes 31457284 | tf_op jit(solution)/shard_map/while
  155.3 4.2 %copy-start.5 = (bf16[256,512]{0,1:T(8,128)(2,1)S(1)}, bf16[256,512]{0,1:T(8,128)(2,1)}, u32[]{:S(2)}) copy-start(bf16[256,512]{0,1:T(8,128)(2,1)} %get-tuple-element.194) | copy-start | bytes 786436 | tf_op jit(solution)/shard_map/while
  179.6 4.0 %copy-start.2 = (bf16[2,128,8,64]{1,0,3,2:T(2,128)(2,1)S(1)}, bf16[2,128,8,64]{1,0,3,2:T(2,128)(2,1)}, u32[]{:S(2)}) copy-start(bf16[2,128,8,64]{1,0,3,2:T(2,128)(2,1)} %reshape.441) | copy-start | bytes 786436 | tf_op jit(solution)/shard_map/while
  183.5 8.1 %copy-start.3 = (bf16[1280,512]{0,1:T(8,128)(2,1)S(1)}, bf16[1280,512]{0,1:T(8,128)(2,1)}, u32[]{:S(2)}) copy-start(bf16[1280,512]{0,1:T(8,128)(2,1)} %get-tuple-element.187) | copy-start | bytes 3932164 | tf_op jit(solution)/shard_map/while
  185.2 7.0 %copy-start.1 = (f32[8,2,128,1280]{3,2,1,0:T(8,128)S(1)}, f32[8,2,128,1280]{3,2,1,0:T(8,128)}, u32[]{:S(2)}) copy-start(f32[8,2,128,1280]{3,2,1,0:T(8,128)} %get-tuple-element.189) | copy-start | bytes 31457284 | tf_op jit(solution)/shard_map/while
  192.1 4.2 %copy-start.5 = (bf16[256,512]{0,1:T(8,128)(2,1)S(1)}, bf16[256,512]{0,1:T(8,128)(2,1)}, u32[]{:S(2)}) copy-start(bf16[256,512]{0,1:T(8,128)(2,1)} %get-tuple-element.194) | copy-start | bytes 786436 | tf_op jit(solution)/shard_map/while
  (6 other events, 12.5 us)
